TPU v7x, 32 devices: a whole 2x2x4 slice. The times are simulated.
32 devices in a mesh: grp: 4 (over z), row: 8 (over y, x, core).
Axes of the slice: x: 2, y: 2, z: 4, core: 2. Of those that a mesh axis runs over, the one named last changes fastest.
Arguments:
- a_pieces: bfloat16 [4, 512, 4096], P('grp', 'row'), as said below
- touched: int32 [4, 512], P('grp', 'row'), may hold values from 0 to 7
- slot_row: int32 [512], P('row'), may hold values from 0 to 511, as said below
- x_blocks: bfloat16 [32, 64, 64], P('grp'), as said below
- z_inverse: bfloat16 [32, 64, 64], P('grp'), as said below
- block_class: int32 [32], P('grp'), may hold values from 0 to 1
Outputs:
- schur: float32 [512, 512], P('row', 'grp')
Inputs may be any that keep to these rules, and one draw needn't show every extreme that they name: `slot_row`: A permutation of the constraints. The 64 slots of one index r of row (slots r * 64 onward) hold, of the constraints o * 64 to (o + 1) * 64 - 1 of each index o, either none or exactly 16. `a_pieces`: each piece read as a 64 x 64 matrix is symmetric. `x_blocks`: each block is symmetric positive definite. `z_inverse`: each block is symmetric positive definite.
All inputs are finite; a program needn't handle non-finite values.
Results may differ from a plain program's by a relative error of at most 0.0008.
Values may be sent and summed in bfloat16 or wider, within the bound.
A program may use at most 64 MiB of HBM per device.

v0:
```python
import jax
import jax.numpy as jnp
from jax import lax
from jax.sharding import PartitionSpec as P


def masked_blocks(blocks, block_class):
    block_order = blocks.shape[1]
    positions = jnp.arange(block_order)
    active = block_order // 2 * (1 + block_class)
    inside = (positions[None, :, None] < active[:, None, None]) & (
        positions[None, None, :] < active[:, None, None]
    )
    return jnp.where(inside, blocks, jnp.zeros_like(blocks))


def shards(a_pieces, touched, slot_row, x_blocks, z_inverse, block_class):
    local_rows = a_pieces.shape[1]
    block_order = x_blocks.shape[1]
    flat_len = a_pieces.shape[2]
    x_masked = masked_blocks(x_blocks, block_class)
    z_masked = masked_blocks(z_inverse, block_class)
    own_block = touched[0]
    a_local = a_pieces[0]
    pieces = a_local.reshape(local_rows, block_order, block_order)
    left_part = jnp.einsum(
        "rab,rbc->rac", x_masked[own_block], pieces, preferred_element_type=jnp.float32
    ).astype(jnp.bfloat16)
    product = jnp.einsum(
        "rab,rbc->rac", left_part, z_masked[own_block], preferred_element_type=jnp.float32
    ).astype(jnp.bfloat16)
    product_flat = product.reshape(local_rows, flat_len)
    all_slots, all_kinds = (
        lax.all_gather(slot_row, "row", axis=0, tiled=True),
        lax.all_gather(touched, "row", axis=1, tiled=True),
    )
    constraints = all_slots.shape[0]
    kinds_flat = all_kinds[0]
    scores = lax.dot_general(
        product_flat,
        lax.all_gather(a_local, "row", axis=0, tiled=True),
        (((1,), (1,)), ((), ())),
        preferred_element_type=jnp.float32,
    )
    scores = jnp.where(own_block[:, None] == kinds_flat[None, :], scores, jnp.zeros_like(scores))
    inverse = (
        jnp.zeros((constraints,), jnp.int32)
        .at[all_slots]
        .set(jnp.arange(constraints, dtype=jnp.int32))
    )
    ordered = scores[:, inverse]
    summed = lax.psum_scatter(ordered, "grp", scatter_dimension=1, tiled=True)
    columns = summed.shape[1]
    devices = lax.axis_size("row")
    slot_cap = max(2, local_rows // devices * 2)
    owners = slot_row // local_rows
    earlier = jnp.arange(local_rows)[None, :] < jnp.arange(local_rows)[:, None]
    rank_send = jnp.sum(((owners[:, None] == owners[None, :]) & earlier).astype(jnp.int32), axis=1)
    send_slot = owners * slot_cap + rank_send
    outgoing = jnp.zeros((devices * slot_cap, columns), jnp.float32).at[send_slot].set(summed)
    incoming = lax.all_to_all(outgoing, "row", split_axis=0, concat_axis=0, tiled=True)
    my_row = lax.axis_index("row")
    table_ids = all_slots.reshape(devices, local_rows)
    arrives = table_ids // local_rows == my_row
    rank_recv = jnp.cumsum(arrives.astype(jnp.int32), axis=1) - 1
    source_base = (jnp.arange(devices, dtype=jnp.int32) * slot_cap)[:, None]
    target = jnp.where(arrives, source_base + rank_recv, devices * slot_cap)
    landing = jnp.full((devices * slot_cap + 1,), local_rows, jnp.int32)
    landing = landing.at[target.reshape(-1)].set((table_ids % local_rows).reshape(-1))
    result = (
        jnp.zeros((local_rows, columns), jnp.float32).at[landing[:-1]].set(incoming, mode="drop")
    )
    return result


def solution(mesh):
    return jax.shard_map(
        shards,
        mesh=mesh,
        in_specs=(
            P("grp", "row", None),
            P("grp", "row"),
            P("row"),
            P("grp", None, None),
            P("grp", None, None),
            P("grp"),
        ),
        out_specs=P("row", "grp"),
        check_vma=False,
    )
```

profile of v0, /device:TPU:0, one launch (start us, length us, event | category | flops | bytes accessed | tf_op | source)
XLA Modules:
  0.0 93.4 jit_solution(4507066098227181438)
XLA Ops:
  6.5 0.7 all-gather.3.cloned.1.call-update
  7.3 0.0 reduce-scatter.2.cloned.1.call-start
  7.3 2.1 %reshape_squeeze.3 = bf16[64,64,64]{2,1,0:T(8,128)(2,1)S(1)} reshape(bf16[1,64,4096]{2,1,0:T(8,128)(2,1)} %param.6) | data formatting | bytes 1048576 | tf_op jit(solution)/shard_map/reshape;squeeze | solution.py:25
  9.4 1.2 %dynamic-slice = u32[1]{0:T(128)} dynamic-slice(u32[32]{0:T(128)} %constant.77, u32[]{:T(128)S(6)} %add.84), dynamic_slice_sizes={1} | dynamic-slice | bytes 12
  11.3 0.9 dynamic-update-slice
  12.1 0.7 bitcast_dynamic-update-slice_fusion
  12.9 9.5 %all-reduce.2 = (s32[512]{0:T(512)S(1)}, s32[512]{0:T(512)S(1)}) all-reduce(s32[512]{0:T(512)S(1)} %dynamic-update-slice, s32[512]{0:T(512)S(1)} %bitcast_dynamic-update-slice_fusion), channel_id=1, replica_groups=mesh['grp'=4,'row'=8] {'row'}, use_global_device_ids=true, to_apply=%add | all-reduce | flops 1024 | bytes 8192
  22.4 0.1 reshape.95
  22.5 0.2 reduce_window_sum.11
  22.7 0.1 add_add_fusion
  22.8 0.1 add.71
  22.8 0.7 fusion.18
  23.5 0.7 add_multiply_fusion
  24.2 0.1 iota_compare_fusion.1
  24.2 1.1 %and_select_fusion.1 = (bf16[8,64,64]{2,1,0:T(8,128)(2,1)S(1)}, bf16[8,64,64]{2,1,0:T(8,128)(2,1)S(1)}) fusion(bf16[8,64,64]{2,1,0:T(8,128)(2,1)} %param.9, pred[8,64]{1,0:T(8,128)(4,1)S(1)} %iota_compare_fusion.1, bf16[8,64,64]{2,1,0:T(8,128)(2,1)} %param.10), kind=kLoop, calls=%fused_computation.13 | loop fusion | flops 98304 | bytes 262656 | tf_op jit(solution)/shard_map/jit(_where)/select_n | solution.py:14
  25.4 0.7 gather_fusion.1
  26.1 0.7 gather_fusion
  26.9 1.7 %convolution_convert_fusion = bf16[64,64,64]{2,1,0:T(8,128)(2,1)} fusion(bf16[64,64,64]{2,1,0:T(8,128)(2,1)S(1)} %gather_fusion.1, bf16[64,64,64]{2,1,0:T(8,128)(2,1)S(1)} %gather_fusion, bf16[64,64,64]{2,1,0:T(8,128)(2,1)S(1)} %reshape_squeeze.3), kind=kOutput, calls=%fused_computation.9 | convolution fusion | flops 67633152 | bytes 2097152 | tf_op jit(solution)/shard_map/rab,rbc->rac/dot_general | solution.py:29
  28.6 2.1 %reshape.96 = bf16[64,4096]{1,0:T(8,128)(2,1)S(1)} reshape(bf16[64,64,64]{2,1,0:T(8,128)(2,1)} %convolution_convert_fusion) | data formatting | bytes 1048576 | tf_op jit(solution)/shard_map/reshape | solution.py:32
  30.7 2.4 %scatter_custom_fusion.1 = s32[512]{0:T(512)S(1)} fusion(s32[512]{0:T(512)S(1)} %get-tuple-element.7, s32[512]{0:T(512)S(1)} %iota.33, s32[]{:T(128)} %constant.35.clone.1), kind=kCustom, calls=%fused_computation.52 | custom fusion | bytes 2052 | tf_op jit(solution)/shard_map/scatter | solution.py:49
  33.2 15.4 %all-gather.3.cloned.1.call-done = bf16[1,512,4096]{2,1,0:T(8,128)(2,1)} async-done(((bf16[1,64,4096]{2,1,0:T(8,128)(2,1)}), bf16[1,512,4096]{2,1,0:T(8,128)(2,1)}) %all-gather.3.cloned.1.call-update) | async-done | bytes 4194320 | tf_op jit(solution)/shard_map/all_gather | solution.py:41
  48.6 3.6 %fusion.2 = f32[64,512]{1,0:T(8,128)S(1)} fusion(bf16[64,4096]{1,0:T(8,128)(2,1)S(1)} %reshape.96, bf16[1,512,4096]{2,1,0:T(8,128)(2,1)} %all-gather.3.cloned.1.call-done, s32[512]{0:T(512)S(1)} %get-tuple-element.6, s32[64]{0:T(128)S(1)} %bitcast.21), kind=kOutput, calls=%fused_computation.11 | convolution fusion | flops 268500992 | bytes 4851968 | tf_op jit(solution)/shard_map/dot_general | solution.py:39
  52.2 0.1 copy.10
  52.3 1.6 %gather_fusion.2 = f32[512,64]{1,0:T(8,128)} fusion(f32[64,512]{0,1:T(8,128)S(1)} %copy.10, s32[1024]{0:T(1024)S(1)} %pad_clamp_fusion), kind=kCustom, calls=%fused_computation.2 | custom fusion | bytes 264192 | tf_op jit(solution)/shard_map/gather | solution.py:51
  54.0 0.2 convert_reduce_fusion
  54.2 2.4 %scatter_custom_fusion = s32[129]{0:T(256)S(1)} fusion(s32[512]{0:T(512)S(1)} %get-tuple-element.9, s32[512]{0:T(512)S(1)} %get-tuple-element.8, s32[]{:T(128)} %constant.33.clone.1), kind=kCustom, calls=%fused_computation.58 | custom fusion | bytes 520 | tf_op jit(solution)/shard_map/scatter | solution.py:69
  56.6 17.5 %reduce-scatter.2.cloned.1.call-done = f32[64,128]{0,1:T(8,128)} async-done(((f32[64,512]{0,1:T(8,128)}), f32[64,128]{0,1:T(8,128)}) %reduce-scatter.2.cloned.1.call-update) | async-done | bytes 32784 | tf_op jit(solution)/shard_map/reduce_scatter | solution.py:52
  74.1 0.9 copy.11
  75.0 1.3 %scatter_custom_fusion.2 = f32[128,128]{1,0:T(8,128)} fusion(s32[64]{0:T(128)S(1)} %compare_select_fusion.3, f32[64,128]{1,0:T(8,128)S(1)} %copy.11, f32[]{:T(128)} %constant.31.clone.1), kind=kCustom, calls=%fused_computation.16 | custom fusion | bytes 65540 | tf_op jit(solution)/shard_map/scatter | solution.py:60
  76.4 3.7 %all-to-all-start = ((f32[8,16,128]{2,1,0:T(8,128)}), f32[8,16,128]{2,1,0:T(8,128)S(1)}, u32[]{:S(2)}, u32[]{:S(2)}) async-start(f32[8,16,128]{2,1,0:T(8,128)} %bitcast.6), calls=%async_computation.1 | async-start | bytes 131072 | tf_op jit(solution)/shard_map/all_to_all | solution.py:61
  80.1 5.0 %all-to-all-done = f32[8,16,128]{2,1,0:T(8,128)S(1)} async-done(((f32[8,16,128]{2,1,0:T(8,128)}), f32[8,16,128]{2,1,0:T(8,128)S(1)}, u32[]{:S(2)}, u32[]{:S(2)}) %all-to-all-start) | async-done | bytes 65568 | tf_op jit(solution)/shard_map/all_to_all | solution.py:61
  85.1 1.4 %scatter_custom_fusion.3 = f32[64,128]{1,0:T(8,128)} fusion(s32[128]{0:T(128)S(1)} %compare_select_fusion.4, f32[128,128]{1,0:T(8,128)S(1)} %bitcast.20, f32[]{:T(128)} %constant.31.clone.1), kind=kCustom, calls=%fused_computation.19 | custom fusion | bytes 32772 | tf_op jit(solution)/shard_map/scatter | solution.py:71
  (18 shorter events, 0.1 us)
Async XLA Ops:
  6.5 42.1 %all-gather.3.cloned.1.call-start = ((), (), s32[]{:S(2)}) async-start(), calls=%async_computation.3 | async-start | bytes 4718592 | tf_op jit(solution)/shard_map/all_gather | solution.py:41
  7.3 66.9 %reduce-scatter.2.cloned.1.call-start = ((), (), s32[]{:S(2)}) async-start(), calls=%async_computation.2 | async-start | bytes 327680 | tf_op jit(solution)/shard_map/reduce_scatter | solution.py:52
  26.1 7.0 %copy-start.1 = (s32[64]{0:T(128)S(1)}, s32[64]{0:T(128)}, u32[]{:S(2)}) copy-start(s32[64]{0:T(128)} %param.8) | copy-start | bytes 772
  26.1 22.5 %copy-start = (s32[1,64]{1,0:T(1,128)S(1)}, s32[1,64]{1,0:T(1,128)}, u32[]{:S(2)}) copy-start(s32[1,64]{1,0:T(1,128)} %param.7) | copy-start | bytes 772
  76.4 8.7 %all-to-all-start = ((f32[8,16,128]{2,1,0:T(8,128)}), f32[8,16,128]{2,1,0:T(8,128)S(1)}, u32[]{:S(2)}, u32[]{:S(2)}) async-start(f32[8,16,128]{2,1,0:T(8,128)} %bitcast.6), calls=%async_computation.1 | async-start | bytes 131072 | tf_op jit(solution)/shard_map/all_to_all | solution.py:61
Sparse Core Ops, SparseCore 0:
  9.2 39.3 all-gather.2
  54.1 19.9 reduce-scatter.1
where the time goes:
time: 93.7 us; the launch traced here: 93.4 us
  waiting for transfers between devices  38.7 us (41%)
  local copies, waits for them, and re-layouts  19 us (20%)
  between operations  14.2 us (15%)
  blocking collectives  9.49 us (10%)
  matrix products  5.27 us (6%)
  starting transfers between devices  3.72 us (4%)
  other arithmetic  3.04 us (3%)
    reduce_scatter x1, waiting for transfers between devices, shards(): summed = lax.psum_scatter(ordered, 'grp', scatter_dimension=1, tiled=True)  17.5 us
    all_gather x1, waiting for transfers between devices, shards(): lax.all_gather(a_local, 'row', axis=0, tiled=True)  15.4 us
    unnamed x1, blocking collectives  9.49 us
    all_to_all x1, waiting for transfers between devices, shards(): lax.all_to_all(outgoing, 'row', split_axis=0, concat_axis=0, tiled=True)  5.01 us
    all_to_all x1, starting transfers between devices, shards(): lax.all_to_all(outgoing, 'row', split_axis=0, concat_axis=0, tiled=True)  3.68 us
    dot_general x1, matrix products, shards(): lax.dot_general(product_flat, lax.all_gather(a_local, 'row', axis=0, tile...  3.58 us
    unnamed x9, local copies, waits for them, and re-layouts  2.86 us
    scatter x1, local copies, waits for them, and re-layouts, shards(): landing.at[target.reshape(-1)].set((table_ids % local_rows).reshape(-1))  2.44 us
  transfers between devices with their start and end apart: 3, of which 3 were waited for; matrix products, arithmetic and copies ran while one was open for 20% of the time, Pallas kernels for 0%

commit v1 on v0

--- a/solution.py
+++ b/solution.py
@@ -38,7 +38,9 @@
     kinds_flat = all_kinds[0]
     scores = lax.dot_general(
         product_flat,
-        lax.all_gather(a_local, "row", axis=0, tiled=True),
+        jnp.concatenate(
+            lax.all_to_all(jnp.stack([a_local] * lax.axis_size("row")), "row", 0, 0), axis=0
+        ),
         (((1,), (1,)), ((), ())),
         preferred_element_type=jnp.float32,
     )

time: 93.7 us -> 121 us (1.29)
  blocking collectives: 9.49 us -> 48.5 us
  waiting for transfers between devices: 38.7 us -> 22.7 us
  starting transfers between devices: 3.72 us -> 9.03 us
  other arithmetic: 3.04 us -> 1.43 us
    unnamed x1, blocking collectives: 9.49 us -> 48.5 us
    all_gather x1 -> x0, waiting for transfers between devices: 15.4 us -> none  [shards(): lax.all_gather(a_local, 'row', axis=0, tiled=True)]
    all_to_all x0 -> x1, starting transfers between devices: none -> 5.34 us  [shards(): lax.all_to_all(jnp.stack([a_local] * lax.axis_size('row')), 'row', 0, 0)]
    another operation x0 -> x1, local copies, waits for them, and re-layouts: none -> 3.54 us  [shards(): jnp.stack([a_local] * lax.axis_size('row'))]
    unnamed x9 -> x21, local copies, waits for them, and re-layouts: 2.86 us -> 0.95 us
  transfers between devices with their start and end apart: 3 -> 3, of which waited for: 3 -> 2; matrix products, arithmetic and copies ran while one was open for 20% -> 11% of each run, Pallas kernels for 0% -> 0%
where the time goes in v1:
time: 121 us
  blocking collectives  48.5 us (40%)
  waiting for transfers between devices  22.7 us (19%)
  local copies, waits for them, and re-layouts  19.7 us (16%)
  between operations  14.3 us (12%)
  starting transfers between devices  9.03 us (7%)
  matrix products  5.39 us (4%)
  other arithmetic  1.43 us (1%)
    unnamed x1, blocking collectives  48.5 us
    reduce_scatter x1, waiting for transfers between devices, shards(): summed = lax.psum_scatter(ordered, 'grp', scatter_dimension=1, tiled=True)  17.7 us
    all_to_all x1, starting transfers between devices, shards(): lax.all_to_all(jnp.stack([a_local] * lax.axis_size('row')), 'row', 0, 0)  5.34 us
    all_to_all x1, waiting for transfers between devices, shards(): lax.all_to_all(outgoing, 'row', split_axis=0, concat_axis=0, tiled=True)  5.01 us
    all_to_all x1, starting transfers between devices, shards(): lax.all_to_all(outgoing, 'row', split_axis=0, concat_axis=0, tiled=True)  3.65 us
    dot_general x1, matrix products, shards(): lax.dot_general(product_flat, jnp.concatenate(lax.all_to_all(jnp.stack([a...  3.59 us
    another operation x1, local copies, waits for them, and re-layouts, shards(): jnp.stack([a_local] * lax.axis_size('row'))  3.54 us
    scatter x1, local copies, waits for them, and re-layouts, shards(): landing.at[target.reshape(-1)].set((table_ids % local_rows).reshape(-1))  2.44 us
  transfers between devices with their start and end apart: 3, of which 2 were waited for; matrix products, arithmetic and copies ran while one was open for 11% of the time, Pallas kernels for 0%

profile of v1, /device:TPU:0, one launch (start us, length us, event | category | flops | bytes accessed | tf_op | source)
XLA Modules:
  0.0 121.0 jit_solution(15557534788435186210)
XLA Ops:
  6.5 3.5 %stack.3 = bf16[8,64,4096]{2,1,0:T(8,128)(2,1)} broadcast(bf16[64,4096]{1,0:T(8,128)(2,1)} %bitcast.17), dimensions={1,2} | broadcast | bytes 4718592 | tf_op jit(solution)/shard_map/stack | solution.py:42
  10.1 5.3 %all-to-all-start = ((bf16[8,64,4096]{2,1,0:T(8,128)(2,1)}), bf16[8,64,4096]{2,1,0:T(8,128)(2,1)}, u32[]{:S(2)}, u32[]{:S(2)}) async-start(bf16[8,64,4096]{2,1,0:T(8,128)(2,1)} %stack.3), calls=%async_computation | async-start | bytes 8388608 | tf_op jit(solution)/shard_map/all_to_all | solution.py:42
  15.5 0.0 reduce-scatter.2.cloned.1.call-start
  15.5 1.1 reshape_squeeze.3
  16.7 0.6 dynamic-slice
  17.9 0.2 dynamic-update-slice
  18.2 0.1 bitcast_dynamic-update-slice_fusion
  18.3 48.5 %all-reduce.2 = (s32[512]{0:T(512)S(1)}, s32[512]{0:T(512)S(1)}) all-reduce(s32[512]{0:T(512)S(1)} %dynamic-update-slice, s32[512]{0:T(512)S(1)} %bitcast_dynamic-update-slice_fusion), channel_id=1, replica_groups=mesh['grp'=4,'row'=8] {'row'}, use_global_device_ids=true, to_apply=%add | all-reduce | flops 1024 | bytes 8192
  66.8 0.1 reshape.99
  66.9 0.2 reduce_window_sum.11
  67.1 0.1 add_add_fusion
  67.2 0.1 add.71
  67.3 0.1 iota_compare_fusion.1
  67.4 0.1 and_select_fusion.1
  67.5 0.7 gather_fusion.1
  68.3 0.7 gather_fusion
  69.0 1.8 %convolution_convert_fusion = bf16[64,64,64]{2,1,0:T(8,128)(2,1)} fusion(bf16[64,64,64]{2,1,0:T(8,128)(2,1)S(1)} %gather_fusion.1, bf16[64,64,64]{2,1,0:T(8,128)(2,1)S(1)} %gather_fusion, bf16[64,64,64]{2,1,0:T(8,128)(2,1)S(1)} %reshape_squeeze.3), kind=kOutput, calls=%fused_computation.7 | convolution fusion | flops 67633152 | bytes 2097152 | tf_op jit(solution)/shard_map/rab,rbc->rac/dot_general | solution.py:29
  70.9 2.1 %reshape.100 = bf16[64,4096]{1,0:T(8,128)(2,1)S(1)} reshape(bf16[64,64,64]{2,1,0:T(8,128)(2,1)} %convolution_convert_fusion) | data formatting | bytes 1048576 | tf_op jit(solution)/shard_map/reshape | solution.py:32
  73.0 2.4 %scatter_custom_fusion.1 = s32[512]{0:T(512)S(1)} fusion(s32[512]{0:T(512)S(1)} %get-tuple-element.7, s32[512]{0:T(512)S(1)} %iota.33, s32[]{:T(128)} %constant.35.clone.1), kind=kCustom, calls=%fused_computation.50 | custom fusion | bytes 2052 | tf_op jit(solution)/shard_map/scatter | solution.py:51
  75.4 0.7 and_select_fusion.2
  76.1 3.6 %convolution_select_fusion = f32[64,512]{1,0:T(8,128)S(1)} fusion(bf16[64,4096]{1,0:T(8,128)(2,1)S(1)} %reshape.100, bf16[512,4096]{1,0:T(8,128)(2,1)} %bitcast.5, s32[512]{0:T(512)S(1)} %get-tuple-element.6, s32[64]{0:T(128)} %bitcast.20), kind=kOutput, calls=%fused_computation.9 | convolution fusion | flops 268500992 | bytes 4851968 | tf_op jit(solution)/shard_map/dot_general | solution.py:39
  79.7 0.1 copy.10
  79.8 1.6 %gather_fusion.2 = f32[512,64]{1,0:T(8,128)} fusion(f32[64,512]{0,1:T(8,128)S(1)} %copy.10, s32[1024]{0:T(1024)S(1)} %pad_clamp_fusion), kind=kCustom, calls=%fused_computation.2 | custom fusion | bytes 264192 | tf_op jit(solution)/shard_map/gather | solution.py:53
  81.5 0.0 reduce-scatter.2.cloned.1.call-update
  81.5 0.2 convert_reduce_fusion
  81.7 2.4 %scatter_custom_fusion = s32[129]{0:T(256)S(1)} fusion(s32[512]{0:T(512)S(1)} %get-tuple-element.9, s32[512]{0:T(512)S(1)} %get-tuple-element.8, s32[]{:T(128)} %constant.33.clone.1), kind=kCustom, calls=%fused_computation.56 | custom fusion | bytes 520 | tf_op jit(solution)/shard_map/scatter | solution.py:71
  84.1 17.7 %reduce-scatter.2.cloned.1.call-done = f32[64,128]{0,1:T(8,128)} async-done(((f32[64,512]{0,1:T(8,128)}), f32[64,128]{0,1:T(8,128)}) %reduce-scatter.2.cloned.1.call-update) | async-done | bytes 32784 | tf_op jit(solution)/shard_map/reduce_scatter | solution.py:54
  101.9 0.9 copy.11
  102.8 1.3 %scatter_custom_fusion.2 = f32[128,128]{1,0:T(8,128)} fusion(s32[64]{0:T(128)S(1)} %compare_select_fusion.3, f32[64,128]{1,0:T(8,128)S(1)} %copy.11, f32[]{:T(128)} %constant.31.clone.1), kind=kCustom, calls=%fused_computation.14 | custom fusion | bytes 65540 | tf_op jit(solution)/shard_map/scatter | solution.py:62
  104.1 3.6 %all-to-all-start.1 = ((f32[8,16,128]{2,1,0:T(8,128)}), f32[8,16,128]{2,1,0:T(8,128)S(1)}, u32[]{:S(2)}, u32[]{:S(2)}) async-start(f32[8,16,128]{2,1,0:T(8,128)} %bitcast.7), calls=%async_computation.2 | async-start | bytes 131072 | tf_op jit(solution)/shard_map/all_to_all | solution.py:63
  107.7 5.0 %all-to-all-done.1 = f32[8,16,128]{2,1,0:T(8,128)S(1)} async-done(((f32[8,16,128]{2,1,0:T(8,128)}), f32[8,16,128]{2,1,0:T(8,128)S(1)}, u32[]{:S(2)}, u32[]{:S(2)}) %all-to-all-start.1) | async-done | bytes 65568 | tf_op jit(solution)/shard_map/all_to_all | solution.py:63
  112.8 1.4 %scatter_custom_fusion.3 = f32[64,128]{1,0:T(8,128)} fusion(s32[128]{0:T(128)S(1)} %compare_select_fusion.4, f32[128,128]{1,0:T(8,128)S(1)} %bitcast.19, f32[]{:T(128)} %constant.31.clone.1), kind=kCustom, calls=%fused_computation.17 | custom fusion | bytes 32772 | tf_op jit(solution)/shard_map/scatter | solution.py:73
  (30 shorter events, 0.1 us)
Async XLA Ops:
  10.1 5.4 %copy-start = (bf16[1,64,4096]{2,1,0:T(8,128)(2,1)S(1)}, bf16[1,64,4096]{2,1,0:T(8,128)(2,1)}, u32[]{:S(2)}) copy-start(bf16[1,64,4096]{2,1,0:T(8,128)(2,1)} %param.6) | copy-start | bytes 1572868
  10.1 6.6 %copy-start.7 = (u32[32]{0:T(128)S(1)}, u32[32]{0:T(128)}, u32[]{:S(2)}) copy-start(u32[32]{0:T(128)} %constant.77) | copy-start | bytes 388
  10.1 7.8 %copy-start.5 = (s32[64]{0:T(128)S(1)}, s32[64]{0:T(128)}, u32[]{:S(2)}) copy-start(s32[64]{0:T(128)} %param.8) | copy-start | bytes 772
  10.1 8.1 %copy-start.3 = (s32[1,64]{1,0:T(1,128)S(1)}, s32[1,64]{1,0:T(1,128)}, u32[]{:S(2)}) copy-start(s32[1,64]{1,0:T(1,128)} %param.7) | copy-start | bytes 772
  10.1 57.2 %copy-start.4 = (s32[8]{0:T(128)S(1)}, s32[8]{0:T(128)}, u32[]{:S(2)}) copy-start(s32[8]{0:T(128)} %param.11) | copy-start | bytes 100
  10.1 57.3 %copy-start.1 = (bf16[8,64,64]{2,1,0:T(8,128)(2,1)S(1)}, bf16[8,64,64]{2,1,0:T(8,128)(2,1)}, u32[]{:S(2)}) copy-start(bf16[8,64,64]{2,1,0:T(8,128)(2,1)} %param.9) | copy-start | bytes 196612
  10.1 57.3 %copy-start.2 = (bf16[8,64,64]{2,1,0:T(8,128)(2,1)S(1)}, bf16[8,64,64]{2,1,0:T(8,128)(2,1)}, u32[]{:S(2)}) copy-start(bf16[8,64,64]{2,1,0:T(8,128)(2,1)} %param.10) | copy-start | bytes 196612
  10.1 66.0 %all-to-all-start = ((bf16[8,64,4096]{2,1,0:T(8,128)(2,1)}), bf16[8,64,4096]{2,1,0:T(8,128)(2,1)}, u32[]{:S(2)}, u32[]{:S(2)}) async-start(bf16[8,64,4096]{2,1,0:T(8,128)(2,1)} %stack.3), calls=%async_computation | async-start | bytes 8388608 | tf_op jit(solution)/shard_map/all_to_all | solution.py:42
  15.5 86.4 %reduce-scatter.2.cloned.1.call-start = ((), (), s32[]{:S(2)}) async-start(), calls=%async_computation.3 | async-start | bytes 327680 | tf_op jit(solution)/shard_map/reduce_scatter | solution.py:54
  70.8 13.3 %copy-start.6 = (s32[64]{0:T(128)S(1)}, s32[64]{0:T(128)}, u32[]{:S(2)}) copy-start(s32[64]{0:T(128)} %param.8) | copy-start | bytes 772
  104.1 8.7 %all-to-all-start.1 = ((f32[8,16,128]{2,1,0:T(8,128)}), f32[8,16,128]{2,1,0:T(8,128)S(1)}, u32[]{:S(2)}, u32[]{:S(2)}) async-start(f32[8,16,128]{2,1,0:T(8,128)} %bitcast.7), calls=%async_computation.2 | async-start | bytes 131072 | tf_op jit(solution)/shard_map/all_to_all | solution.py:63
Sparse Core Ops, SparseCore 0:
  81.6 20.1 reduce-scatter.1
